TPU v7x, 32 devices: a whole 2x2x4 slice. The times are simulated.
32 devices in a mesh: dp: 16 (over z, y, x), mp: 2 (over core).
Axes of the slice: x: 2, y: 2, z: 4, core: 2. Of those that a mesh axis runs over, the one named last changes fastest.
Arguments:
- hidden: bfloat16 [4096, 8192], P('dp', 'mp'), may hold values from -6 to 6
- w_key: bfloat16 [8192, 1024], P('mp', 'dp'), may hold values from -0.0625 to 0.0625
- w_value: bfloat16 [8192, 1024], P('mp', 'dp'), may hold values from -0.0625 to 0.0625
- queries: bfloat16 [4096, 8192], P('dp', 'mp'), may hold values from -150 to 150
- lengths: int32 [16], replicated, may hold values from 1 to 512, as said below
- seq_of_slot: int32 [32], replicated, may hold values from 0 to 15, as said below
- pos_of_slot: int32 [32], replicated, may hold values from 0 to 3, as said below
Outputs:
- context: bfloat16 [4096, 8192], P('dp', 'mp')
- key_cache: bfloat16 [16, 512, 1024], P('dp', None, 'mp')
- value_cache: bfloat16 [16, 512, 1024], P('dp', None, 'mp')
Inputs may be any that keep to these rules, and one draw needn't show every extreme that they name: Sequence q has ceil(lengths[q] / 128) blocks, 1 to 4; some sequence has 4 full blocks. `seq_of_slot`: slots 2 i and 2 i + 1 belong to replica i. Every block of every sequence stands in exactly one slot. The blocks of one sequence stand on different replicas; the two slots of a replica hold blocks of different sequences; and for any two replicas A and B, at most one block on A is an earlier block of the same sequence as some block on B. `pos_of_slot`: given with seq_of_slot: the block index, from 0, of the block in each slot.
All inputs are finite; a program needn't handle non-finite values.
Results may differ from a plain program's by a relative error of at most 0.011.
Values may be sent and summed in bfloat16 or wider, within the bound.
A program may use at most 128 MiB of HBM per device.

v0:
```python
import functools
import math

import jax
import jax.numpy as jnp
from jax import lax
from jax.experimental import pallas as pl
from jax.experimental.pallas import tpu as pltpu
from jax.sharding import PartitionSpec as P

HQ = 64
KVH = 8
HD = 128
BLOCK = 128
MAXB = 4


def rotate(field, positions):
    halfway = field.shape[-1] // 2
    indices = jnp.arange(halfway, dtype=jnp.float32)
    frequency = jnp.exp(-(2.0 * indices / field.shape[-1]) * math.log(500000.0))
    angles = positions[:, None] * frequency[None, :]
    cosines = jnp.cos(angles)[:, None, :]
    sines = jnp.sin(angles)[:, None, :]
    front = field[..., :halfway]
    back = field[..., halfway:]
    return jnp.concatenate(
        [front * cosines - back * sines, back * cosines + front * sines], axis=-1
    )


def shards(hidden, w_key, w_value, queries, lengths, seq_of_slot, pos_of_slot):
    replica = lax.axis_index("dp")
    token_rows = hidden.shape[0]
    local_slots = token_rows // BLOCK
    key_full, value_full = (
        lax.all_gather(w_key, "dp", axis=1, tiled=True),
        lax.all_gather(w_value, "dp", axis=1, tiled=True),
    )
    key_sum = jnp.dot(hidden, key_full, preferred_element_type=jnp.float32)
    value_sum = jnp.dot(hidden, value_full, preferred_element_type=jnp.float32)
    key_raw, value_raw = (
        lax.psum_scatter(key_sum, "mp", scatter_dimension=1, tiled=True),
        lax.psum_scatter(value_sum, "mp", scatter_dimension=1, tiled=True),
    )
    head_width = key_raw.shape[1]
    local_heads = head_width // HD
    my_seq = lax.dynamic_slice_in_dim(seq_of_slot, replica * local_slots, local_slots)
    my_pos = lax.dynamic_slice_in_dim(pos_of_slot, replica * local_slots, local_slots)
    offsets = jnp.arange(BLOCK, dtype=jnp.int32)
    query_pos = my_pos[:, None] * BLOCK + offsets[None, :]
    key_rows = rotate(
        key_raw.reshape(token_rows, local_heads, HD),
        query_pos.reshape(token_rows).astype(jnp.float32),
    )
    key_rows = key_rows.reshape(token_rows, head_width).astype(jnp.bfloat16)
    value_rows = value_raw.astype(jnp.bfloat16)
    payload = jnp.concatenate([key_rows, value_rows], axis=1).reshape(
        local_slots, BLOCK * 2 * head_width
    )
    blocks = jnp.arange(MAXB, dtype=jnp.int32)
    needed = (
        (seq_of_slot[None, None, :] == my_seq[:, None, None])
        & (pos_of_slot[None, None, :] == blocks[None, :, None])
        & (blocks[None, :, None] < my_pos[:, None, None])
    )
    owned = (seq_of_slot[None, :] == replica) & (pos_of_slot[None, :] == blocks[:, None])
    needed_pick = needed.astype(jnp.bfloat16)
    owned_pick = owned.astype(jnp.bfloat16)
    portion = lax.all_gather(payload, "dp", axis=0, tiled=True)
    earlier = jnp.einsum("smn,nx->smx", needed_pick, portion, preferred_element_type=jnp.float32)
    home_rows = jnp.dot(owned_pick, portion, preferred_element_type=jnp.float32)
    own_block = (blocks[None, :] == my_pos[:, None]).astype(jnp.float32)
    assembled = (earlier + own_block[:, :, None] * payload[:, None, :].astype(jnp.float32)).astype(
        jnp.bfloat16
    )
    span = MAXB * BLOCK
    assembled = assembled.reshape(local_slots, span, 2 * head_width)
    key_blocks = assembled[:, :, :head_width].reshape(local_slots, span, local_heads, HD)
    value_blocks = assembled[:, :, head_width:].reshape(local_slots, span, local_heads, HD)
    ratio = HQ // KVH
    query_blocks = queries.reshape(local_slots, BLOCK, local_heads, ratio, HD)
    scores = jnp.einsum(
        "sbgrd,scgd->sgrbc", query_blocks, key_blocks, preferred_element_type=jnp.float32
    ) * (1.0 / math.sqrt(HD))
    slot_lengths = lengths[my_seq]
    cached = jnp.arange(span, dtype=jnp.int32)
    allowed = (cached[None, None, :] <= query_pos[:, :, None]) & (
        cached[None, None, :] < slot_lengths[:, None, None]
    )
    scores = jnp.where(allowed[:, None, None], scores, -1e30)
    largest = jnp.max(scores, axis=-1, keepdims=True)
    weights = jnp.exp(scores - largest)
    probs = (weights / jnp.sum(weights, axis=-1, keepdims=True)).astype(jnp.bfloat16)
    mixed = jnp.einsum("sgrbc,scgd->sbgrd", probs, value_blocks, preferred_element_type=jnp.float32)
    valid = query_pos < slot_lengths[:, None]
    mixed = jnp.where(valid[:, :, None, None, None], mixed, 0.0)
    context = mixed.reshape(token_rows, local_heads * ratio * HD).astype(jnp.bfloat16)
    cache_rows = home_rows.reshape(span, 2 * head_width)
    own_length = lax.dynamic_slice_in_dim(lengths, replica, 1)[0]
    cache_rows = jnp.where((cached < own_length)[:, None], cache_rows, 0.0).astype(jnp.bfloat16)
    return (context, cache_rows[None, :, :head_width], cache_rows[None, :, head_width:])


MESH = pl.DeviceIdType.MESH
PAYLOAD_ORDERS = (("z", "x", "y"), ("y", "z", "x"), ("x", "y", "z"))
PAYLOAD_PARTS = (5, 3, 1)
HIDDEN_ORDERS = (("x", "y"), ("y", "x"))
HIDDEN_PARTS = (5, 3)
TILE = 16
PAIR = 2


def cut(rows, weights):
    tiles = rows // TILE
    sizes, done = [], 0
    for i, w in enumerate(weights):
        upto = tiles * sum(weights[: i + 1]) // sum(weights)
        sizes.append((done * TILE, (upto - done) * TILE))
        done = upto
    return sizes


def guarded(conditions, action):
    live = [c for c in conditions if c is not None]
    if not live:
        action()
        return
    test = live[0]
    for c in live[1:]:
        test = jnp.logical_and(test, c)
    pl.when(test)(action)


class Gather:
    def __init__(self, place, depth, view, orders, recv_sem, send_sem):
        self.place, self.depth, self.view = place, depth, view
        self.recv_sem, self.send_sem = recv_sem, send_sem
        self.sends = []
        found = []
        for part, order in enumerate(orders):
            reach = [(0, 0, 0, -1, 0)]
            for step, dim in enumerate(order):
                fresh = []
                for rx, ry, dz, _, hops in reach:
                    if dim == "x":
                        fresh.append((1, ry, dz, step, hops + 1))
                    elif dim == "y":
                        fresh.append((rx, 1, dz, step, hops + 1))
                    else:
                        for k in range(1, depth):
                            fresh.append((rx, ry, -k, step, hops + k))
                            fresh.append((rx, ry, k, step, hops + k))
                reach += fresh
            found += [(hops, part, order, step, rx, ry, dz) for rx, ry, dz, step, hops in reach]
        self.found = sorted(found, key=lambda f: (self.final(f), f[0], f[3] - len(f[2])))
        self.slot = {(f[1], f[4], f[5], f[6]): i for i, f in enumerate(self.found)}

    @staticmethod
    def final(entry):
        _, _, order, step, _, _, _ = entry
        return step == len(order) - 1 and order[step] != "z"

    @staticmethod
    def counts(depth, orders):
        pieces = sends = 0
        for order in orders:
            n = 1
            for dim in order:
                n *= 2 if dim in "xy" else 2 * depth - 1
            pieces += n
            sends += 3 * n
        return pieces, sends

    def exists(self, dz):
        z = self.place[2]
        if dz < 0:
            return z + dz >= 0
        if dz > 0:
            return z + dz < self.depth
        return None

    def ref(self, part, rx, ry, dz):
        x, y, z, _ = self.place
        ox = 1 - x if rx else x
        oy = 1 - y if ry else y
        return self.view(part, ox, oy, z + dz)

    def target(self, dim, sign):
        x, y, z, c = self.place
        if dim == "x":
            x = 1 - x
        elif dim == "y":
            y = 1 - y
        else:
            z = z + sign
        return ((z * 2 + y) * 2 + x, c)

    def send(self, part, rx, ry, dz, dim, sign):
        there = (part, rx ^ (dim == "x"), ry ^ (dim == "y"), dz - sign if dim == "z" else dz)
        if there not in self.slot:
            return
        z = self.place[2]
        conditions = [self.exists(dz)]
        if dim == "z":
            conditions.append(z + sign < self.depth if sign > 0 else z + sign >= 0)
        block = self.ref(part, rx, ry, dz)
        copy = pltpu.make_async_remote_copy(
            src_ref=block,
            dst_ref=block,
            send_sem=self.send_sem.at[len(self.sends)],
            recv_sem=self.recv_sem.at[self.slot[there]],
            device_id=self.target(dim, sign),
            device_id_type=MESH,
        )
        self.sends.append((conditions, copy))
        guarded(conditions, copy.start)

    def onward(self, entry):
        _, part, order, step, rx, ry, dz = entry
        if step >= 0 and order[step] == "z":
            self.send(part, rx, ry, dz, "z", 1 if dz < 0 else -1)
        for dim in order[step + 1 :]:
            if dim == "z":
                self.send(part, rx, ry, dz, "z", 1)
                self.send(part, rx, ry, dz, "z", -1)
            else:
                self.send(part, rx, ry, dz, dim, 0)

    def arrive(self, entry):
        _, part, order, step, rx, ry, dz = entry
        block = self.ref(part, rx, ry, dz)
        copy = pltpu.make_async_remote_copy(
            src_ref=block,
            dst_ref=block,
            send_sem=self.send_sem.at[0],
            recv_sem=self.recv_sem.at[self.slot[(part, rx, ry, dz)]],
            device_id=self.target("x", 0),
            device_id_type=MESH,
        )
        guarded([self.exists(dz)], copy.wait_recv)

    def own(self):
        return [f for f in self.found if f[0] == 0]

    def rest(self):
        return [f for f in self.found if f[0] > 0]

    def drain(self):
        for conditions, copy in self.sends:
            guarded(conditions, copy.wait_send)


def exchange_kernel(
    depth,
    hidden_ref,
    pack_ref,
    cos_ref,
    sin_ref,
    kv_ref,
    hid,
    packs,
    give,
    full,
    acc,
    peer,
    local_sem,
    swap_sem,
    peer_send,
    peer_recv,
    hid_recv,
    hid_send,
    w_recv,
    w_send,
    kv_recv,
    kv_send,
):
    me = lax.axis_index("dp")
    core = lax.axis_index("mp")
    x = me % 2
    y = (me // 2) % 2
    z = me // 4
    place = (x, y, z, core)
    rows = hidden_ref.shape[0]
    mine = y * 2 + x
    across = (z * 4 + y * 2 + (1 - x), core)
    along = (z * 4 + (1 - y) * 2 + x, core)
    other = (me, 1 - core)

    local = [
        pltpu.make_async_copy(hidden_ref, hid.at[mine], local_sem.at[0]),
        pltpu.make_async_copy(pack_ref.at[0], packs.at[z, x], local_sem.at[1]),
        pltpu.make_async_copy(pack_ref.at[1], give, local_sem.at[2]),
    ]
    for copy in local:
        copy.start()
    barrier = pltpu.get_barrier_semaphore()

    def greet(device):
        pl.semaphore_signal(barrier, inc=1, device_id=device, device_id_type=MESH)

    for device in (across, along, other):
        greet(device)
    pl.when(z > 0)(lambda: greet((me - 4, core)))
    pl.when(z < depth - 1)(lambda: greet((me + 4, core)))
    inner = jnp.logical_and(z > 0, z < depth - 1)
    pl.when(inner)(lambda: pl.semaphore_wait(barrier, 5))
    pl.when(jnp.logical_not(inner))(lambda: pl.semaphore_wait(barrier, 4 if depth > 1 else 3))
    for copy in local:
        copy.wait()

    swap = pltpu.make_async_remote_copy(
        src_ref=give,
        dst_ref=packs.at[z, x],
        send_sem=swap_sem.at[0],
        recv_sem=swap_sem.at[1],
        device_id=across,
        device_id_type=MESH,
    )
    swap.start()

    spans = cut(rows, HIDDEN_PARTS)

    def hid_view(part, ox, oy, oz):
        return hid.at[oy * 2 + ox, pl.ds(*spans[part])]

    def w_view(part, ox, oy, oz):
        half = x if part == 0 else 1 - x
        return packs.at[oz, half]

    hidden_gather = Gather(place, depth, hid_view, HIDDEN_ORDERS, hid_recv, hid_send)
    w_gather = Gather(place, depth, w_view, (("z",), ("z",)), w_recv, w_send)
    w_own = w_gather.own()
    w_gather.onward(w_own[0])
    for entry in hidden_gather.own():
        hidden_gather.onward(entry)
    swap.wait_recv()
    w_gather.onward(w_own[1])
    events = [(2.0 * f[0] - 1 + f[1], 0, f) for f in w_gather.rest()]
    events += [
        (100.0 if Gather.final(f) else 3.5 + 0.7 * f[1], 1, f) for f in hidden_gather.rest()
    ]
    for _, which, entry in sorted(events, key=lambda e: e[0]):
        gather = (w_gather, hidden_gather)[which]
        gather.arrive(entry)
        gather.onward(entry)

    width = packs.shape[3] // 2
    span = packs.shape[2]
    for k in range(depth):
        h0 = packs[k, 0]
        h1 = packs[k, 1]
        columns = pl.ds(k * 2 * width, 2 * width)
        full[pl.ds(0, span), columns] = jnp.concatenate([h0[:, :width], h1[:, :width]], axis=1)
        full[pl.ds(span, span), columns] = jnp.concatenate([h0[:, width:], h1[:, width:]], axis=1)

    half_width = acc.shape[2]
    sends = []
    for i in range(4):
        block = pl.ds(i * rows, rows)
        for h in range(2):
            acc[h, block] = jnp.dot(
                hid[i],
                full[:, pl.ds(h * half_width, half_width)],
                preferred_element_type=jnp.float32,
            )
        copy = pltpu.make_async_remote_copy(
            src_ref=acc.at[1 - core, block],
            dst_ref=peer.at[block],
            send_sem=peer_send.at[i],
            recv_sem=peer_recv.at[i],
            device_id=other,
            device_id_type=MESH,
        )
        copy.start()
        sends.append(copy)

    heads = half_width // HD
    for i in range(4):
        sends[i].wait_recv()
        block = pl.ds(i * rows, rows)
        cosines = cos_ref[block]
        sines = sin_ref[block]
        for h in range(heads):
            columns = pl.ds(h * HD, HD)
            total = acc[core, block, columns] + peer[block, columns]
            turned = total * cosines + pltpu.roll(total, HD // 2, 1) * sines
            kv_ref[me, block, columns] = turned.astype(jnp.bfloat16)

    kv_spans = cut(kv_ref.shape[1], PAYLOAD_PARTS)

    def kv_view(part, ox, oy, oz):
        return kv_ref.at[(oz * 2 + oy) * 2 + ox, pl.ds(*kv_spans[part])]

    kv_gather = Gather(place, depth, kv_view, PAYLOAD_ORDERS, kv_recv, kv_send)
    for entry in kv_gather.own():
        kv_gather.onward(entry)
    for entry in kv_gather.rest():
        kv_gather.arrive(entry)
        kv_gather.onward(entry)

    swap.wait_send()
    for copy in sends:
        copy.wait_send()
    hidden_gather.drain()
    w_gather.drain()
    kv_gather.drain()


def attend_kernel(ratio, local_slots, tab_ref, q_ref, *refs):
    blocks, out_ref = refs[:MAXB], refs[MAXB]
    s = pl.program_id(0)
    length = tab_ref[local_slots * MAXB + s]
    start = tab_ref[local_slots * (MAXB + 1) + s] * BLOCK
    keys = jnp.concatenate([b[0, 0, 0] for b in blocks], axis=0)
    values = jnp.concatenate([b[0, 0, 1] for b in blocks], axis=0)
    span = keys.shape[0]
    row = start + lax.broadcasted_iota(jnp.int32, (BLOCK, span), 0)
    col = lax.broadcasted_iota(jnp.int32, (BLOCK, span), 1)
    bias = jnp.where((col <= row) & (col < length), 0.0, -1e30)
    bias = jnp.concatenate([bias] * PAIR, axis=0)
    valid = (start + lax.broadcasted_iota(jnp.int32, (BLOCK, HD), 0)) < length
    for r in range(0, ratio, PAIR):
        q = jnp.concatenate([q_ref[:, pl.ds((r + i) * HD, HD)] for i in range(PAIR)], axis=0)
        scores = lax.dot_general(
            q, keys, (((1,), (1,)), ((), ())), preferred_element_type=jnp.float32
        )
        scores = scores + bias
        largest = jnp.max(scores, axis=1, keepdims=True)
        weights = jnp.exp2((scores - largest) * (math.log2(math.e) / math.sqrt(HD)))
        scale = 1.0 / jnp.sum(weights, axis=1, keepdims=True)
        mixed = jnp.dot(weights.astype(jnp.bfloat16), values, preferred_element_type=jnp.float32)
        mixed = mixed * scale
        for i in range(PAIR):
            part = jnp.where(valid, mixed[i * BLOCK : (i + 1) * BLOCK], 0.0)
            out_ref[:, pl.ds((r + i) * HD, HD)] = part.astype(jnp.bfloat16)


def cache_kernel(local_heads, tab_ref, kv_ref, key_ref, value_ref):
    m = pl.program_id(0)
    length = tab_ref[MAXB]
    place = m * BLOCK + lax.broadcasted_iota(jnp.int32, (BLOCK, HD), 0)
    for g in range(local_heads):
        columns = pl.ds(g * HD, HD)
        inner = pl.ds(g // 2 * HD, HD)
        for which, out in ((0, key_ref), (1, value_ref)):
            block = kv_ref[0, g % 2, which, :, inner]
            out[0, :, columns] = jnp.where(place < length, block, jnp.zeros_like(block))


def fast_shards(hidden, w_key, w_value, queries, lengths, seq_of_slot, pos_of_slot):
    replica = lax.axis_index("dp")
    depth = lax.axis_size("dp") // 4
    rows, features = hidden.shape
    width = w_key.shape[1]
    plane = 4 * rows
    plane_slots = plane // BLOCK
    half_width = depth * width
    local_heads = 2 * half_width // HD
    x = replica % 2
    middle = features // 2
    k_pack = jnp.concatenate([w_key[:middle], w_key[middle:]], axis=1)
    v_pack = jnp.concatenate([w_value[:middle], w_value[middle:]], axis=1)
    pack = jnp.stack([jnp.where(x == 0, k_pack, v_pack), jnp.where(x == 0, v_pack, k_pack)])

    plane_pos = lax.dynamic_slice_in_dim(pos_of_slot, replica // 4 * plane_slots, plane_slots)
    positions = (plane_pos[:, None] * BLOCK + jnp.arange(BLOCK, dtype=jnp.int32)[None, :]).reshape(plane)
    lane = jnp.arange(HD, dtype=jnp.int32)
    indices = (lane % (HD // 2)).astype(jnp.float32)
    frequency = jnp.exp(-(2.0 * indices / HD) * math.log(500000.0))
    angles = positions.astype(jnp.float32)[:, None] * frequency[None, :]
    cosines = jnp.where(x == 0, jnp.cos(angles), 1.0)
    sines = jnp.sin(angles)
    sines = jnp.where(x == 0, jnp.where(lane[None, :] < HD // 2, -sines, sines), 0.0)

    hid_counts = Gather.counts(depth, HIDDEN_ORDERS)
    w_counts = Gather.counts(depth, (("z",), ("z",)))
    kv_counts = Gather.counts(depth, PAYLOAD_ORDERS)
    dma = pltpu.SemaphoreType.DMA
    vmem = pl.BlockSpec(memory_space=pltpu.VMEM)
    anywhere = pl.BlockSpec(memory_space=pl.ANY)
    kv = pl.pallas_call(
        functools.partial(exchange_kernel, depth),
        out_shape=jax.ShapeDtypeStruct((4 * depth, plane, half_width), jnp.bfloat16),
        in_specs=[anywhere, anywhere, vmem, vmem],
        out_specs=vmem,
        scratch_shapes=[
            pltpu.VMEM((4, rows, features), jnp.bfloat16),
            pltpu.VMEM((depth, 2, middle, 2 * width), jnp.bfloat16),
            pltpu.VMEM((middle, 2 * width), jnp.bfloat16),
            pltpu.VMEM((features, 2 * half_width), jnp.bfloat16),
            pltpu.VMEM((2, plane, half_width), jnp.float32),
            pltpu.VMEM((plane, half_width), jnp.float32),
            dma((3,)),
            dma((2,)),
            dma((4,)),
            dma((4,)),
            dma((hid_counts[0],)),
            dma((hid_counts[1],)),
            dma((w_counts[0],)),
            dma((w_counts[1],)),
            dma((kv_counts[0],)),
            dma((kv_counts[1],)),
        ],
        compiler_params=pltpu.CompilerParams(
            collective_id=0, has_side_effects=True, vmem_limit_bytes=60 * 2**20
        ),
    )(hidden, pack, cosines, sines)
    kv = kv.reshape(depth, 2, 2, plane, half_width)

    slots = rows // BLOCK
    my_seq = lax.dynamic_slice_in_dim(seq_of_slot, replica * slots, slots)
    my_pos = lax.dynamic_slice_in_dim(pos_of_slot, replica * slots, slots)
    wanted = jnp.concatenate([my_seq, replica[None].astype(jnp.int32)])
    blocks = jnp.arange(MAXB, dtype=jnp.int32)
    ids = jnp.arange(seq_of_slot.shape[0], dtype=jnp.int32)
    match = (seq_of_slot[None, None, :] == wanted[:, None, None]) & (
        pos_of_slot[None, None, :] == blocks[None, :, None]
    )
    source = jnp.sum(jnp.where(match, ids[None, None, :], 0), axis=2)
    bounds = jnp.sum(jnp.where(wanted[:, None] == jnp.arange(lengths.shape[0])[None, :], lengths[None, :], 0), axis=1)
    table = jnp.concatenate([source[:slots].reshape(-1), bounds[:slots], my_pos]).astype(jnp.int32)
    home = jnp.concatenate([source[slots], bounds[slots:]]).astype(jnp.int32)

    def block_spec(m):
        def index(s, g, tab):
            slot = tab[s * MAXB + m]
            return (slot // plane_slots, g % 2, 0, slot % plane_slots, g // 2)

        return pl.BlockSpec((1, 1, 2, BLOCK, HD), index)

    group = queries.shape[1] // local_heads
    context = pl.pallas_call(
        functools.partial(attend_kernel, group // HD, slots),
        out_shape=jax.ShapeDtypeStruct(queries.shape, jnp.bfloat16),
        grid_spec=pltpu.PrefetchScalarGridSpec(
            num_scalar_prefetch=1,
            grid=(slots, local_heads),
            in_specs=[pl.BlockSpec((BLOCK, group), lambda s, g, tab: (s, g))]
            + [block_spec(m) for m in range(MAXB)],
            out_specs=pl.BlockSpec((BLOCK, group), lambda s, g, tab: (s, g)),
        ),
    )(table, queries, *([kv] * MAXB))

    cache = jax.ShapeDtypeStruct((1, MAXB * BLOCK, local_heads * HD), jnp.bfloat16)
    cache_spec = pl.BlockSpec((1, BLOCK, local_heads * HD), lambda m, tab: (0, m, 0))
    key_cache, value_cache = pl.pallas_call(
        functools.partial(cache_kernel, local_heads),
        out_shape=(cache, cache),
        grid_spec=pltpu.PrefetchScalarGridSpec(
            num_scalar_prefetch=1,
            grid=(MAXB,),
            in_specs=[
                pl.BlockSpec(
                    (1, 2, 2, BLOCK, half_width),
                    lambda m, tab: (tab[m] // plane_slots, 0, 0, tab[m] % plane_slots, 0),
                )
            ],
            out_specs=(cache_spec, cache_spec),
        ),
    )(home, kv)
    return context, key_cache, value_cache


def suits(mesh):
    replicas, halves = mesh.shape["dp"], mesh.shape["mp"]
    return halves == 2 and replicas % 8 == 0 and KVH * HD == replicas * (HD // 2)


def solution(mesh):
    in_specs = (P("dp", "mp"), P("mp", "dp"), P("mp", "dp"), P("dp", "mp"), P(), P(), P())
    out_specs = (P("dp", "mp"), P("dp", None, "mp"), P("dp", None, "mp"))
    return jax.shard_map(fast_shards if suits(mesh) else shards, mesh=mesh, in_specs=in_specs, out_specs=out_specs, check_vma=False)
```

profile of v0, /device:TPU:0, one launch (start us, length us, event | category | flops | bytes accessed | tf_op | source)
XLA Modules:
  0.0 187.4 jit_solution(14575431114589422599)
XLA Ops:
  0.7 0.8 dynamic-slice_multiply_fusion
  1.5 0.7 dynamic_slice.9
  2.2 0.1 pad_add_fusion
  2.3 0.7 dynamic_slice.10
  3.0 0.8 select_reduce_fusion.1
  3.8 0.6 slice.31
  4.4 0.7 broadcast_compare_fusion
  5.1 0.7 iota_compare_fusion.1
  5.8 0.2 select_reduce_fusion
  6.0 0.1 reshape.213
  6.1 0.6 pad_add_fusion.1.tab_ref
  6.7 1.2 pad_add_fusion.2.tab_ref
  7.9 0.1 convert_bitcast_fusion
  8.0 1.1 fusion.7
  9.0 0.3 copy.18
  9.3 0.3 copy.19
  9.7 0.3 copy.20
  9.9 0.3 copy.21
  10.2 0.6 broadcast_select_fusion.1
  10.9 1.1 pad_maximum_fusion.pack_ref
  11.9 3.1 %fusion.1 = (f32[1024,128]{1,0:T(8,128)}, f32[1024,128]{1,0:T(8,128)}) fusion(f32[128]{0:T(128)S(1)} %fusion.6, f32[1024]{0:T(1024)S(1)} %convert_bitcast_fusion, pred[128]{0:T(512)(128)(4,1)S(1)} %iota_compare_fusion.2, pred[]{:T(512)S(6)} %eq.68), kind=kLoop, calls=%fused_computation.5 | loop fusion | flops 655360 | bytes 1053313 | tf_op jit(solution)/shard_map/jit(_where)/select_n | solution.py:474
  15.0 154.0 %shard_map.94 = bf16[16,1024,256]{2,1,0:T(8,128)(2,1)} custom-call(bf16[256,4096]{1,0:T(8,128)(2,1)} %hidden_ref.1, bf16[2,2048,128]{2,1,0:T(8,128)(2,1)} %pad_maximum_fusion.pack_ref, f32[1024,128]{1,0:T(8,128)} %get-tuple-element.14.cos_ref, f32[1024,128]{1,0:T(8,128)} %get-tuple-element.13.sin_ref), custom_call_target="tpu_custom_call" | custom-call | tf_op jit(solution)/shard_map/pallas_call | solution.py:482
  169.1 3.3 %shard_map.96 = (bf16[1,512,512]{2,1,0:T(8,128)(2,1)}, bf16[1,512,512]{2,1,0:T(8,128)(2,1)}) custom-call(s32[5]{0:T(128)} %pad_add_fusion.2.tab_ref, bf16[4,2,2,1024,256]{4,3,2,1,0:T(8,128)(2,1)} %bitcast.11), custom_call_target="tpu_custom_call" | custom-call | tf_op jit(solution)/shard_map/pallas_call | solution.py:547
  172.3 15.1 %shard_map.95 = bf16[256,4096]{1,0:T(8,128)(2,1)} custom-call(s32[12]{0:T(128)} %pad_add_fusion.1.tab_ref, bf16[256,4096]{1,0:T(8,128)(2,1)} %q_ref.1, bf16[4,2,2,1024,256]{4,3,2,1,0:T(8,128)(2,1)} %bitcast.12, bf16[4,2,2,1024,256]{4,3,2,1,0:T(8,128)(2,1)} %bitcast.13, bf16[4,2,2,1024,256]{4,3,2,1,0:T(8,128)(2,1)} %bitcast.14, ...), custom_call_target="tpu_custom_call" | custom-call | tf_op jit(solution)/shard_map/pallas_call | solution.py:533
  (7 shorter events, 0.1 us)
Async XLA Ops:
  0.6 9.0 %copy-start = (bf16[4096,64]{0,1:T(8,128)(2,1)S(1)}, bf16[4096,64]{0,1:T(8,128)(2,1)}, u32[]{:S(2)}) copy-start(bf16[4096,64]{0,1:T(8,128)(2,1)} %param.9) | copy-start | bytes 1572868
where the time goes:
time: 188 us; the launch traced here: 187 us
  Pallas kernels  172 us (91%)
  other arithmetic  9.95 us (5%)
  local copies, waits for them, and re-layouts  4.34 us (2%)
    pallas_call x1, Pallas kernels, fast_shards(): pl.pallas_call(functools.partial(exchange_kernel, depth), out_shape=jax.S...  154 us
    pallas_call x1, Pallas kernels, fast_shards(): pl.pallas_call(functools.partial(attend_kernel, group // HD, slots), out_...  15.1 us

commit v1 on v0

v1 whole, which is shorter than its diff:
```python
import functools
import math

import jax
import jax.numpy as jnp
from jax import lax
from jax.experimental import pallas as pl
from jax.experimental.pallas import tpu as pltpu
from jax.sharding import PartitionSpec as P

HQ = 64
KVH = 8
HD = 128
BLOCK = 128
MAXB = 4


def rotate(field, positions):
    halfway = field.shape[-1] // 2
    indices = jnp.arange(halfway, dtype=jnp.float32)
    frequency = jnp.exp(-(2.0 * indices / field.shape[-1]) * math.log(500000.0))
    angles = positions[:, None] * frequency[None, :]
    cosines = jnp.cos(angles)[:, None, :]
    sines = jnp.sin(angles)[:, None, :]
    front = field[..., :halfway]
    back = field[..., halfway:]
    return jnp.concatenate(
        [front * cosines - back * sines, back * cosines + front * sines], axis=-1
    )


def shards(hidden, w_key, w_value, queries, lengths, seq_of_slot, pos_of_slot):
    replica = lax.axis_index("dp")
    token_rows = hidden.shape[0]
    local_slots = token_rows // BLOCK
    key_full, value_full = (
        lax.all_gather(w_key, "dp", axis=1, tiled=True),
        lax.all_gather(w_value, "dp", axis=1, tiled=True),
    )
    key_sum = jnp.dot(hidden, key_full, preferred_element_type=jnp.float32)
    value_sum = jnp.dot(hidden, value_full, preferred_element_type=jnp.float32)
    key_raw, value_raw = (
        lax.psum_scatter(key_sum, "mp", scatter_dimension=1, tiled=True),
        lax.psum_scatter(value_sum, "mp", scatter_dimension=1, tiled=True),
    )
    head_width = key_raw.shape[1]
    local_heads = head_width // HD
    my_seq = lax.dynamic_slice_in_dim(seq_of_slot, replica * local_slots, local_slots)
    my_pos = lax.dynamic_slice_in_dim(pos_of_slot, replica * local_slots, local_slots)
    offsets = jnp.arange(BLOCK, dtype=jnp.int32)
    query_pos = my_pos[:, None] * BLOCK + offsets[None, :]
    key_rows = rotate(
        key_raw.reshape(token_rows, local_heads, HD),
        query_pos.reshape(token_rows).astype(jnp.float32),
    )
    key_rows = key_rows.reshape(token_rows, head_width).astype(jnp.bfloat16)
    value_rows = value_raw.astype(jnp.bfloat16)
    payload = jnp.concatenate([key_rows, value_rows], axis=1).reshape(
        local_slots, BLOCK * 2 * head_width
    )
    blocks = jnp.arange(MAXB, dtype=jnp.int32)
    needed = (
        (seq_of_slot[None, None, :] == my_seq[:, None, None])
        & (pos_of_slot[None, None, :] == blocks[None, :, None])
        & (blocks[None, :, None] < my_pos[:, None, None])
    )
    owned = (seq_of_slot[None, :] == replica) & (pos_of_slot[None, :] == blocks[:, None])
    needed_pick = needed.astype(jnp.bfloat16)
    owned_pick = owned.astype(jnp.bfloat16)
    portion = lax.all_gather(payload, "dp", axis=0, tiled=True)
    earlier = jnp.einsum("smn,nx->smx", needed_pick, portion, preferred_element_type=jnp.float32)
    home_rows = jnp.dot(owned_pick, portion, preferred_element_type=jnp.float32)
    own_block = (blocks[None, :] == my_pos[:, None]).astype(jnp.float32)
    assembled = (earlier + own_block[:, :, None] * payload[:, None, :].astype(jnp.float32)).astype(
        jnp.bfloat16
    )
    span = MAXB * BLOCK
    assembled = assembled.reshape(local_slots, span, 2 * head_width)
    key_blocks = assembled[:, :, :head_width].reshape(local_slots, span, local_heads, HD)
    value_blocks = assembled[:, :, head_width:].reshape(local_slots, span, local_heads, HD)
    ratio = HQ // KVH
    query_blocks = queries.reshape(local_slots, BLOCK, local_heads, ratio, HD)
    scores = jnp.einsum(
        "sbgrd,scgd->sgrbc", query_blocks, key_blocks, preferred_element_type=jnp.float32
    ) * (1.0 / math.sqrt(HD))
    slot_lengths = lengths[my_seq]
    cached = jnp.arange(span, dtype=jnp.int32)
    allowed = (cached[None, None, :] <= query_pos[:, :, None]) & (
        cached[None, None, :] < slot_lengths[:, None, None]
    )
    scores = jnp.where(allowed[:, None, None], scores, -1e30)
    largest = jnp.max(scores, axis=-1, keepdims=True)
    weights = jnp.exp(scores - largest)
    probs = (weights / jnp.sum(weights, axis=-1, keepdims=True)).astype(jnp.bfloat16)
    mixed = jnp.einsum("sgrbc,scgd->sbgrd", probs, value_blocks, preferred_element_type=jnp.float32)
    valid = query_pos < slot_lengths[:, None]
    mixed = jnp.where(valid[:, :, None, None, None], mixed, 0.0)
    context = mixed.reshape(token_rows, local_heads * ratio * HD).astype(jnp.bfloat16)
    cache_rows = home_rows.reshape(span, 2 * head_width)
    own_length = lax.dynamic_slice_in_dim(lengths, replica, 1)[0]
    cache_rows = jnp.where((cached < own_length)[:, None], cache_rows, 0.0).astype(jnp.bfloat16)
    return (context, cache_rows[None, :, :head_width], cache_rows[None, :, head_width:])


MESH = pl.DeviceIdType.MESH
PIECES = 4
PAIR = 2
NEAR = (0, -1, 1)
UNITS = ((0, 2), (2, 6), (0, 4))


def when_all(conditions, action):
    live = [c for c in conditions if c is not None]
    if not live:
        action()
        return
    test = live[0]
    for c in live[1:]:
        test = jnp.logical_and(test, c)
    pl.when(test)(action)


def rebuild_kernel(
    depth,
    hidden_ref,
    wk_ref,
    wv_ref,
    q_ref,
    len_ref,
    seq_ref,
    pos_ref,
    ctx_out,
    key_out,
    value_out,
    hid,
    wt,
    acc,
    peer,
    xs,
    xr,
    kv0,
    kv1,
    sel,
    home_sel,
    arr0,
    arr1,
    home0,
    home1,
    qv,
    ctx0,
    ctx1,
    kc,
    vc,
    cos_t,
    sin_t,
    local_sem,
    send_sem,
    w_recv,
    h_recv,
    p_recv,
    x_recv,
    z_recv,
    u_recv,
):
    me = lax.axis_index("dp")
    core = lax.axis_index("mp")
    x = me % 2
    y = (me // 2) % 2
    z = me // 4
    mine = y * 2 + x
    rows = hidden_ref.shape[0]
    feats = hid.shape[2]
    wide = wk_ref.shape[0]
    kvs = (kv0, kv1)
    ctxs = (ctx0, ctx1)
    arrs = (arr0, arr1)
    homes = (home0, home1)
    slots = rows // BLOCK
    plane_slots = 4 * slots
    across = (z * 4 + y * 2 + (1 - x), core)
    along = (z * 4 + (1 - y) * 2 + x, core)
    diagonal = (z * 4 + (1 - y) * 2 + (1 - x), core)
    other = (me, 1 - core)
    targets = (across, along, diagonal)
    plane_ids = (y * 2 + 1 - x, (1 - y) * 2 + x, (1 - y) * 2 + 1 - x)
    my_feats = pl.ds(pl.multiple_of(x * feats, 128), feats)
    nbr_feats = pl.ds(pl.multiple_of((1 - x) * feats, 128), feats)
    sends = []

    def up():
        return z + 1 < depth

    def down():
        return z > 0

    def exists(dz):
        if dz == 0:
            return None
        return z + dz < depth if dz > 0 else z + dz >= 0

    def to_z(sign):
        return (me + 4 * sign, core)

    def remote(src, dst, sem, device):
        copy = pltpu.make_async_remote_copy(
            src_ref=src,
            dst_ref=dst,
            send_sem=send_sem.at[len(sends)],
            recv_sem=sem,
            device_id=device,
            device_id_type=MESH,
        )
        return copy

    def send(conditions, src, dst, sem, device):
        copy = remote(src, dst, sem, device)
        sends.append((conditions, copy))
        when_all(conditions, copy.start)

    def arrived(conditions, dst, sem):
        copy = pltpu.make_async_remote_copy(
            src_ref=dst,
            dst_ref=dst,
            send_sem=send_sem.at[0],
            recv_sem=sem,
            device_id=across,
            device_id_type=MESH,
        )
        when_all(conditions, copy.wait_recv)

    def w_piece(zc, kv, side):
        half = x if side == 0 else 1 - x
        return wt.at[zc, pl.ds(pl.multiple_of(kv * 2 * wide + half * wide, wide), wide)]

    def w_sem(zc, kv, side):
        return w_recv.at[zc * 4 + kv * 2 + side]

    half_q = qv.shape[2]
    order = (1 - core, core)
    local = []
    for i, (src, dst) in enumerate(
        [
            (hidden_ref.at[:, my_feats], hid.at[mine]),
            (wk_ref.at[:, my_feats], w_piece(z, 0, 0)),
            (wv_ref.at[:, my_feats], w_piece(z, 1, 0)),
        ]
        + [
            (q_ref.at[:, pl.ds(pl.multiple_of(order[j] * half_q, 128), half_q)], qv.at[j])
            for j in range(2)
        ]
    ):
        copy = pltpu.make_async_copy(src, dst, local_sem.at[i])
        copy.start()
        local.append(copy)

    barrier = pltpu.get_barrier_semaphore()

    def greet(device):
        pl.semaphore_signal(barrier, inc=1, device_id=device, device_id_type=MESH)

    for device in (across, along, diagonal, other):
        greet(device)
    pl.when(down())(lambda: greet(to_z(-1)))
    pl.when(up())(lambda: greet(to_z(1)))
    inner = jnp.logical_and(down(), up())
    pl.when(inner)(lambda: pl.semaphore_wait(barrier, 6))
    pl.when(jnp.logical_not(inner))(lambda: pl.semaphore_wait(barrier, 5))

    weights = (wk_ref, wv_ref)
    for kv in range(2):
        send([up()], weights[kv].at[:, my_feats], w_piece(z, kv, 0), w_sem(z, kv, 0), to_z(1))
        send([down()], weights[kv].at[:, my_feats], w_piece(z, kv, 0), w_sem(z, kv, 0), to_z(-1))
        give = wt.at[z, pl.ds(pl.multiple_of(kv * 2 * wide + x * wide, wide), wide)]
        send([], weights[kv].at[:, nbr_feats], give, w_sem(z, kv, 1), across)
    step = rows // PIECES
    for p in range(PIECES):
        part = pl.ds(p * step, step)
        send([], hidden_ref.at[part, nbr_feats], hid.at[mine, part], h_recv.at[mine * PIECES + p], across)
        send([], hidden_ref.at[part, my_feats], hid.at[mine, part], h_recv.at[mine * PIECES + p], along)

    total_slots = base = seq_ref.shape[0]
    replicas = [z * 4 + i for i in plane_ids] + [me]
    wanted = []
    for r in replicas:
        wanted += [seq_ref[r * slots + s] for s in range(slots)] + [r]

    def scan(n, found):
        s, m = seq_ref[n], pos_ref[n]
        weight = jnp.where(m == 0, 1, jnp.where(m == 1, base, jnp.where(m == 2, base**2, base**3)))
        coded = n * weight
        return tuple(f + jnp.where(s == w, coded, 0) for f, w in zip(found, wanted))

    found = (0,) * len(wanted)
    for n in range(total_slots):
        found = scan(n, found)
    picks = []
    for t in range(4):
        codes = found[3 * t : 3 * t + 3]
        early = [(codes[s] // base**m) % base for s in range(slots) for m in range(MAXB - 1)]
        home = [(codes[slots] // base**m) % base for m in range(MAXB)]
        picks.append((early, home))

    def tables():
        lane = lax.broadcasted_iota(jnp.int32, (BLOCK, HD), 1)
        indices = (lane % (HD // 2)).astype(jnp.float32)
        frequency = jnp.exp(-(2.0 * indices / HD) * math.log(500000.0))
        row = lax.broadcasted_iota(jnp.int32, (BLOCK, HD), 0)
        for i in range(plane_slots):
            start = pos_ref[z * plane_slots + i] * BLOCK
            angles = (start + row).astype(jnp.float32) * frequency
            cos_t[pl.ds(i * BLOCK, BLOCK)] = jnp.cos(angles)
            sines = jnp.sin(angles)
            sin_t[pl.ds(i * BLOCK, BLOCK)] = jnp.where(lane < HD // 2, -sines, sines)

    pl.when(x == 0)(tables)

    def w_arrive(dz, side):
        zc = z + dz
        here = exists(dz)
        for kv in range(2):
            piece = w_piece(zc, kv, side)
            sem = w_sem(zc, kv, side)
            arrived([here], piece, sem)
            if dz == 0:
                send([up()], piece, piece, sem, to_z(1))
                send([down()], piece, piece, sem, to_z(-1))
            elif abs(dz) < depth - 1:
                sign = 1 if dz < 0 else -1
                send([here, up() if sign > 0 else down()], piece, piece, sem, to_z(sign))

    def h_forward(p):
        part = pl.ds(p * step, step)
        src = plane_ids[0]
        block = hid.at[src, part]
        arrived([], block, h_recv.at[src * PIECES + p])
        send([], block, block, h_recv.at[src * PIECES + p], along)

    w_arrive(0, 1)
    w_arrive(-1, 0)
    w_arrive(1, 0)
    h_forward(0)
    h_forward(1)
    w_arrive(-1, 1)
    w_arrive(1, 1)
    h_forward(2)
    h_forward(3)
    w_arrive(-2, 0)
    w_arrive(2, 0)
    for copy in local:
        copy.wait()
    for p in range(PIECES):
        for src in plane_ids[1:]:
            arrived([], hid.at[src, pl.ds(p * step, step)], h_recv.at[src * PIECES + p])

    def owner(dz):
        return (z + dz) // 2

    def multiply(dz):
        zc = z + dz

        def run():
            for i in range(4):
                block = lax.dot_general(
                    hid[i], wt[zc], (((1,), (1,)), ((), ())), preferred_element_type=jnp.float32
                )
                part = pl.ds(i * rows, rows)
                acc[zc, 0, part] = block[:, :HD]
                acc[zc, 1, part] = block[:, HD:]

        when_all([exists(dz)], run)
        send(
            [exists(dz), owner(dz) != core],
            acc.at[zc],
            peer.at[zc % 2],
            p_recv.at[zc % 2],
            other,
        )

    def reduce(dz):
        zc = z + dz
        k = zc % 2
        mine_here = [exists(dz), owner(dz) == core]
        arrived(mine_here, peer.at[k], p_recv.at[k])

        def body():
            xs[k] = (acc[zc, 1 - x] + peer[k, 1 - x]).astype(jnp.bfloat16)

        when_all(mine_here, body)
        send(mine_here, xs.at[k], xr.at[k], x_recv.at[k], across)

    def finish(dz):
        zc = z + dz
        k = zc % 2
        outer = 1 - ((zc + 1) // 2) % 2
        arrived([exists(dz), owner(dz) == core], xr.at[k], x_recv.at[k])
        for j in range(2):
            kv = kvs[j]
            mine_here = [exists(dz), owner(dz) == core, outer == j]

            def body(kv=kv, j=j):
                for i in range(plane_slots):
                    part = pl.ds(i * BLOCK, BLOCK)
                    total = acc[zc, x, part] + peer[k, x, part] + xr[k, part].astype(jnp.float32)

                    def turn(total=total, part=part, i=i):
                        turned = total * cos_t[part] + pltpu.roll(total, HD // 2, 1) * sin_t[part]
                        kv[z * plane_slots + i] = turned.astype(jnp.bfloat16)

                    def keep(total=total, i=i):
                        kv[z * plane_slots + i] = total.astype(jnp.bfloat16)

                    pl.when(x == 0)(turn)
                    pl.when(x != 0)(keep)

            when_all(mine_here, body)
            block = kv.at[pl.ds(z * plane_slots, plane_slots)]
            send(mine_here + [up()], block, block, z_recv.at[j * depth + z], to_z(1))
            send(mine_here + [down()], block, block, z_recv.at[j * depth + z], to_z(-1))

    def kv_arrive(j, dz):
        here = exists(dz)
        block = kvs[j].at[pl.ds((z + dz) * plane_slots, plane_slots)]
        sem = z_recv.at[j * depth + z + dz]
        sign = 1 if dz < 0 else -1
        onward = up() if sign > 0 else down()
        arrived([here, onward], block, sem)
        if abs(dz) < depth - 1:
            send([here, onward], block, block, sem, to_z(sign))

    def kv_last(j, dz):
        sign = 1 if dz < 0 else -1
        onward = up() if sign > 0 else down()
        block = kvs[j].at[pl.ds((z + dz) * plane_slots, plane_slots)]
        arrived([exists(dz), jnp.logical_not(onward)], block, z_recv.at[j * depth + z + dz])

    def unit_sem(j, t, kind):
        return u_recv.at[(j * 3 + t) * 3 + kind]

    def give_own(j):
        for t in range(3):
            src = kvs[j].at[pl.ds(z * plane_slots + plane_ids[t] * slots, slots)]
            send([], src, arrs[j].at[mine, pl.ds(0, slots)], unit_sem(j, t, 0), targets[t])
        arrs[j][mine, pl.ds(0, slots)] = kvs[j][pl.ds(me * slots, slots)]

    def landing(j, src, kind):
        return (homes if kind == 2 else arrs)[j].at[src, pl.ds(*UNITS[kind])]

    def give_picked(j):
        kv = kvs[j]
        for kind, staged in ((1, sel), (2, home_sel)):
            for t in (2, 0, 1):
                for u in range(UNITS[kind][1]):
                    staged[j, t, u] = kv[picks[t][kind - 1][u]]
                send([], staged.at[j, t], landing(j, mine, kind), unit_sem(j, t, kind), targets[t])
        for u in range(UNITS[1][1]):
            arrs[j][mine, UNITS[1][0] + u] = kv[picks[3][0][u]]
        for u in range(UNITS[2][1]):
            homes[j][mine, u] = kv[picks[3][1][u]]

    def units_arrive(j, kind):
        for t in range(3):
            arrived([], landing(j, plane_ids[t], kind), unit_sem(j, t, kind))

    ratio = half_q // (2 * HD)
    head_span = ratio * HD
    outs = {}

    def copy_out(name, src, dst, sem):
        if name in outs:
            outs[name].wait()
        outs[name] = pltpu.make_async_copy(src, dst, local_sem.at[sem])
        outs[name].start()

    def attend(j):
        units_arrive(j, 0)
        units_arrive(j, 1)
        earlier = MAXB - 1

        def body(i, _):
            s = i // 2
            h = i % 2
            q_pos = pos_ref[me * slots + s]
            length = len_ref[seq_ref[me * slots + s]]
            row = lax.broadcasted_iota(jnp.int32, (BLOCK, BLOCK), 0)
            col = lax.broadcasted_iota(jnp.int32, (BLOCK, BLOCK), 1)
            start = q_pos * BLOCK
            parts = [jnp.where((col <= row) & (start + col < length), 0.0, -1e30)]
            for m in range(earlier):
                parts.append(jnp.full((BLOCK, BLOCK), jnp.where(m < q_pos, 0.0, -1e30), jnp.float32))
            bias = jnp.concatenate(parts, axis=1)
            bias = jnp.concatenate([bias] * PAIR, axis=0)
            valid = (start + row) < length
            span = MAXB * BLOCK
            pieces = []
            for kv in range(2):
                own = arrs[j][2 * h + kv, s]
                rest = arrs[j][2 * h + kv, pl.ds(slots + s * earlier, earlier)]
                pieces.append(
                    jnp.concatenate([own, rest.reshape(earlier * BLOCK, HD)], axis=0)
                )
            keys, values = pieces
            part = pl.ds(pl.multiple_of(s * BLOCK, BLOCK), BLOCK)

            def columns(r):
                return pl.ds(pl.multiple_of(h * head_span + r * HD, HD), HD)

            for r in range(0, ratio, PAIR):
                q = jnp.concatenate([qv[j, part, columns(r + i)] for i in range(PAIR)], axis=0)
                scores = lax.dot_general(
                    q, keys, (((1,), (1,)), ((), ())), preferred_element_type=jnp.float32
                )
                scores = scores + bias
                largest = jnp.max(scores, axis=1, keepdims=True)
                exps = jnp.exp2((scores - largest) * (math.log2(math.e) / math.sqrt(HD)))
                scale = 1.0 / jnp.sum(exps, axis=1, keepdims=True)
                mixed = jnp.dot(exps.astype(jnp.bfloat16), values, preferred_element_type=jnp.float32)
                mixed = mixed * scale
                for i in range(PAIR):
                    piece = jnp.where(valid, mixed[i * BLOCK : (i + 1) * BLOCK], 0.0)
                    ctxs[j][part, columns(r + i)] = piece.astype(jnp.bfloat16)
            return 0

        lax.fori_loop(0, 2 * slots, body, 0)
        target = ctx_out.at[:, pl.ds(pl.multiple_of(order[j] * half_q, 128), half_q)]
        copy_out("context", ctxs[j], target, 5 + j)

    def caches(j):
        units_arrive(j, 2)
        length = len_ref[me]
        for m in range(MAXB):
            place = m * BLOCK + lax.broadcasted_iota(jnp.int32, (BLOCK, HD), 0)
            for h in range(2):
                for kv, out in ((0, kc), (1, vc)):
                    block = homes[j][2 * h + kv, m]
                    out[j, pl.ds(m * BLOCK, BLOCK), pl.ds(h * HD, HD)] = jnp.where(
                        place < length, block, jnp.zeros_like(block)
                    )
        column = pl.ds(pl.multiple_of(order[j] * 2 * HD, 128), 2 * HD)
        copy_out("keys", kc.at[j], key_out.at[0, :, column], 7 + 2 * j)
        copy_out("values", vc.at[j], value_out.at[0, :, column], 8 + 2 * j)

    for dz in NEAR:
        multiply(dz)
    w_arrive(-2, 1)
    w_arrive(2, 1)
    for dz in NEAR:
        reduce(dz)
    multiply(-2)
    multiply(2)
    for dz in NEAR:
        finish(dz)
    for dz in (-2, 2):
        reduce(dz)
    for dz in (-2, 2):
        finish(dz)
    give_own(0)
    for dz in (-1, 1, -2, 2):
        kv_arrive(0, dz)
    w_arrive(-3, 0)
    w_arrive(3, 0)
    w_arrive(-3, 1)
    w_arrive(3, 1)
    for dz in (-3, 3):
        multiply(dz)
    for dz in (-3, 3):
        reduce(dz)
    for dz in (-3, 3):
        finish(dz)
    give_own(1)
    for dz in (-1, 1, -2, 2, -3, 3):
        kv_last(0, dz)
    give_picked(0)
    for dz in (-1, 1, -2, 2):
        kv_arrive(1, dz)
    attend(0)
    caches(0)
    for dz in (-1, 1, -2, 2, -3, 3):
        kv_last(1, dz)
    give_picked(1)
    attend(1)
    caches(1)
    for copy in outs.values():
        copy.wait()
    for conditions, copy in sends:
        when_all(conditions, copy.wait_send)


def fast_shards(hidden, w_key, w_value, queries, lengths, seq_of_slot, pos_of_slot):
    depth = lax.axis_size("dp") // 4
    rows, features = hidden.shape
    wide = w_key.shape[1]
    slots = rows // BLOCK
    local_heads = wide * 4 * depth // HD // 2
    half = features // 2
    total = seq_of_slot.shape[0]
    plane = 4 * rows
    dma = pltpu.SemaphoreType.DMA
    anywhere = pl.BlockSpec(memory_space=pl.ANY)
    smem = pl.BlockSpec(memory_space=pltpu.SMEM)
    cache = jax.ShapeDtypeStruct((1, MAXB * BLOCK, local_heads * HD), jnp.bfloat16)
    bf16, f32 = jnp.bfloat16, jnp.float32
    half_q = queries.shape[1] // 2
    return pl.pallas_call(
        functools.partial(rebuild_kernel, depth),
        out_shape=(jax.ShapeDtypeStruct(queries.shape, bf16), cache, cache),
        in_specs=[anywhere] * 4 + [smem] * 3,
        out_specs=(anywhere,) * 3,
        scratch_shapes=[
            pltpu.VMEM((4, rows, half), bf16),
            pltpu.VMEM((depth, 4 * wide, half), bf16),
            pltpu.VMEM((depth, 2, plane, HD), f32),
            pltpu.VMEM((2, 2, plane, HD), f32),
            pltpu.VMEM((2, plane, HD), bf16),
            pltpu.VMEM((2, plane, HD), bf16),
            pltpu.VMEM((total, BLOCK, HD), bf16),
            pltpu.VMEM((total, BLOCK, HD), bf16),
            pltpu.VMEM((2, 3, 6, BLOCK, HD), bf16),
            pltpu.VMEM((2, 3, 4, BLOCK, HD), bf16),
            pltpu.VMEM((4, 8, BLOCK, HD), bf16),
            pltpu.VMEM((4, 8, BLOCK, HD), bf16),
            pltpu.VMEM((4, 4, BLOCK, HD), bf16),
            pltpu.VMEM((4, 4, BLOCK, HD), bf16),
            pltpu.VMEM((2, rows, half_q), bf16),
            pltpu.VMEM((rows, half_q), bf16),
            pltpu.VMEM((rows, half_q), bf16),
            pltpu.VMEM((2, MAXB * BLOCK, 2 * HD), bf16),
            pltpu.VMEM((2, MAXB * BLOCK, 2 * HD), bf16),
            pltpu.VMEM((plane, HD), f32),
            pltpu.VMEM((plane, HD), f32),
            dma((11,)),
            dma((128,)),
            dma((4 * depth,)),
            dma((4 * PIECES,)),
            dma((2,)),
            dma((2,)),
            dma((2 * depth,)),
            dma((18,)),
        ],
        compiler_params=pltpu.CompilerParams(
            collective_id=0, has_side_effects=True, vmem_limit_bytes=60 * 2**20
        ),
    )(hidden, w_key.T, w_value.T, queries, lengths, seq_of_slot, pos_of_slot)


def suits(mesh):
    replicas, halves = mesh.shape["dp"], mesh.shape["mp"]
    return halves == 2 and replicas % 8 == 0 and KVH * HD == replicas * (HD // 2)


def solution(mesh):
    in_specs = (P("dp", "mp"), P("mp", "dp"), P("mp", "dp"), P("dp", "mp"), P(), P(), P())
    out_specs = (P("dp", "mp"), P("dp", None, "mp"), P("dp", None, "mp"))
    return jax.shard_map(fast_shards if suits(mesh) else shards, mesh=mesh, in_specs=in_specs, out_specs=out_specs, check_vma=False)
```

time: 188 us -> 140 us (0.74)
  Pallas kernels: 172 us -> 134 us
  other arithmetic: 9.95 us -> 0 us
    pallas_call x3 -> x1, Pallas kernels: 172 us -> 134 us  [fast_shards(): pl.pallas_call(functools.partial(rebuild_kernel, depth), out_shape=(jax.S...]
    select_n x2 -> x0, other arithmetic: 3.73 us -> none  [the longest x1 3.09 us: fast_shards(): jnp.where(x == 0, jnp.where(lane[None, :] < HD // 2, -sines, sines), 0.0)]
    unnamed x6 -> x7, local copies, waits for them, and re-layouts: 1.11 us -> 4.81 us
    concatenate x3 -> x0, other arithmetic: 1.91 us -> none  [the longest x1 1.23 us: fast_shards(): home = jnp.concatenate([source[slots], bounds[slots:]]).astype(jnp.int32)]
where the time goes in v1:
time: 140 us
  Pallas kernels  134 us (96%)
  local copies, waits for them, and re-layouts  4.81 us (3%)
    pallas_call x1, Pallas kernels, fast_shards(): pl.pallas_call(functools.partial(rebuild_kernel, depth), out_shape=(jax.S...  134 us
    unnamed x7, local copies, waits for them, and re-layouts  4.81 us

profile of v1, /device:TPU:0, one launch (start us, length us, event | category | flops | bytes accessed | tf_op | source)
XLA Modules:
  0.0 139.9 jit_solution(10211616362739279083)
XLA Ops:
  0.6 134.4 %shard_map.94 = (bf16[256,4096]{1,0:T(8,128)(2,1)}, bf16[1,512,512]{2,1,0:T(8,128)(2,1)}, bf16[1,512,512]{2,1,0:T(8,128)(2,1)}) custom-call(bf16[256,4096]{1,0:T(8,128)(2,1)} %hidden_ref.1, bf16[64,4096]{1,0:T(8,128)(2,1)} %bitcast.2, bf16[64,4096]{1,0:T(8,128)(2,1)} %bitcast.3, bf16[256,4096]{1,0:T(8,128)(2,1)} %q_ref.1, s32[16]{0:T(128)} %len_ref.1, ...), custom_call_target="tpu_custom_call" | custom-call | tf_op jit(solution)/shard_map/pallas_call | solution.py:603
  135.1 0.0 copy-start.1
  135.1 0.0 copy-start
  135.1 3.2 %copy.13 = bf16[256,4096]{1,0:T(8,128)(2,1)} copy(bf16[256,4096]{1,0:T(8,128)(2,1)} %get-tuple-element.6) | data formatting | bytes 4194304
  138.3 0.0 copy-done.1
  138.3 0.8 copy.14
  139.1 0.0 copy-done
  139.1 0.8 copy.15
Async XLA Ops:
  135.1 3.2 %copy-start.1 = (bf16[1,512,512]{2,1,0:T(8,128)(2,1)S(1)}, bf16[1,512,512]{2,1,0:T(8,128)(2,1)}, u32[]{:S(2)}) copy-start(bf16[1,512,512]{2,1,0:T(8,128)(2,1)} %get-tuple-element.7) | copy-start | bytes 1572868
  135.1 4.0 %copy-start = (bf16[1,512,512]{2,1,0:T(8,128)(2,1)S(1)}, bf16[1,512,512]{2,1,0:T(8,128)(2,1)}, u32[]{:S(2)}) copy-start(bf16[1,512,512]{2,1,0:T(8,128)(2,1)} %get-tuple-element.8) | copy-start | bytes 1572868

commit v2 on v1

--- a/solution.py
+++ b/solution.py
@@ -147,10 +147,6 @@
     home0,
     home1,
     qv,
-    ctx0,
-    ctx1,
-    kc,
-    vc,
     cos_t,
     sin_t,
     local_sem,
@@ -172,7 +168,6 @@
     feats = hid.shape[2]
     wide = wk_ref.shape[0]
     kvs = (kv0, kv1)
-    ctxs = (ctx0, ctx1)
     arrs = (arr0, arr1)
     homes = (home0, home1)
     slots = rows // BLOCK
@@ -448,7 +443,7 @@
     def give_picked(j):
         kv = kvs[j]
         for kind, staged in ((1, sel), (2, home_sel)):
-            for t in (2, 0, 1):
+            for t in range(3):
                 for u in range(UNITS[kind][1]):
                     staged[j, t, u] = kv[picks[t][kind - 1][u]]
                 send([], staged.at[j, t], landing(j, mine, kind), unit_sem(j, t, kind), targets[t])
@@ -463,66 +458,55 @@
 
     ratio = half_q // (2 * HD)
     head_span = ratio * HD
-    outs = {}
-
-    def copy_out(name, src, dst, sem):
-        if name in outs:
-            outs[name].wait()
-        outs[name] = pltpu.make_async_copy(src, dst, local_sem.at[sem])
-        outs[name].start()
-
     def attend(j):
-        units_arrive(j, 0)
-        units_arrive(j, 1)
+        for part, head in ((0, y), (1, 1 - y)):
+            for t in range(3)[part : 2 * part + 1]:
+                for kind in range(2):
+                    arrived([], landing(j, plane_ids[t], kind), unit_sem(j, t, kind))
+            lax.fori_loop(0, slots, functools.partial(attend_head, j, head), 0)
+
+    def attend_head(j, h, s, _):
         earlier = MAXB - 1
-
-        def body(i, _):
-            s = i // 2
-            h = i % 2
-            q_pos = pos_ref[me * slots + s]
-            length = len_ref[seq_ref[me * slots + s]]
-            row = lax.broadcasted_iota(jnp.int32, (BLOCK, BLOCK), 0)
-            col = lax.broadcasted_iota(jnp.int32, (BLOCK, BLOCK), 1)
-            start = q_pos * BLOCK
-            parts = [jnp.where((col <= row) & (start + col < length), 0.0, -1e30)]
-            for m in range(earlier):
-                parts.append(jnp.full((BLOCK, BLOCK), jnp.where(m < q_pos, 0.0, -1e30), jnp.float32))
-            bias = jnp.concatenate(parts, axis=1)
-            bias = jnp.concatenate([bias] * PAIR, axis=0)
-            valid = (start + row) < length
-            span = MAXB * BLOCK
-            pieces = []
-            for kv in range(2):
-                own = arrs[j][2 * h + kv, s]
-                rest = arrs[j][2 * h + kv, pl.ds(slots + s * earlier, earlier)]
-                pieces.append(
-                    jnp.concatenate([own, rest.reshape(earlier * BLOCK, HD)], axis=0)
-                )
-            keys, values = pieces
-            part = pl.ds(pl.multiple_of(s * BLOCK, BLOCK), BLOCK)
-
-            def columns(r):
-                return pl.ds(pl.multiple_of(h * head_span + r * HD, HD), HD)
-
-            for r in range(0, ratio, PAIR):
-                q = jnp.concatenate([qv[j, part, columns(r + i)] for i in range(PAIR)], axis=0)
-                scores = lax.dot_general(
-                    q, keys, (((1,), (1,)), ((), ())), preferred_element_type=jnp.float32
-                )
-                scores = scores + bias
-                largest = jnp.max(scores, axis=1, keepdims=True)
-                exps = jnp.exp2((scores - largest) * (math.log2(math.e) / math.sqrt(HD)))
-                scale = 1.0 / jnp.sum(exps, axis=1, keepdims=True)
-                mixed = jnp.dot(exps.astype(jnp.bfloat16), values, preferred_element_type=jnp.float32)
-                mixed = mixed * scale
-                for i in range(PAIR):
-                    piece = jnp.where(valid, mixed[i * BLOCK : (i + 1) * BLOCK], 0.0)
-                    ctxs[j][part, columns(r + i)] = piece.astype(jnp.bfloat16)
-            return 0
-
-        lax.fori_loop(0, 2 * slots, body, 0)
-        target = ctx_out.at[:, pl.ds(pl.multiple_of(order[j] * half_q, 128), half_q)]
-        copy_out("context", ctxs[j], target, 5 + j)
+        q_pos = pos_ref[me * slots + s]
+        length = len_ref[seq_ref[me * slots + s]]
+        row = lax.broadcasted_iota(jnp.int32, (BLOCK, BLOCK), 0)
+        col = lax.broadcasted_iota(jnp.int32, (BLOCK, BLOCK), 1)
+        start = q_pos * BLOCK
+        parts = [jnp.where((col <= row) & (start + col < length), 0.0, -1e30)]
+        for m in range(earlier):
+            parts.append(jnp.full((BLOCK, BLOCK), jnp.where(m < q_pos, 0.0, -1e30), jnp.float32))
+        bias = jnp.concatenate(parts, axis=1)
+        bias = jnp.concatenate([bias] * PAIR, axis=0)
+        valid = (start + row) < length
+        pieces = []
+        for kv in range(2):
+            own = arrs[j][2 * h + kv, s]
+            rest = arrs[j][2 * h + kv, pl.ds(slots + s * earlier, earlier)]
+            pieces.append(jnp.concatenate([own, rest.reshape(earlier * BLOCK, HD)], axis=0))
+        keys, values = pieces
+        part = pl.ds(pl.multiple_of(s * BLOCK, BLOCK), BLOCK)
+        for r in range(0, ratio, PAIR):
+            q = jnp.concatenate(
+                [
+                    qv[j, part, pl.ds(pl.multiple_of(h * head_span + (r + i) * HD, HD), HD)]
+                    for i in range(PAIR)
+                ],
+                axis=0,
+            )
+            scores = lax.dot_general(
+                q, keys, (((1,), (1,)), ((), ())), preferred_element_type=jnp.float32
+            )
+            scores = scores + bias
+            largest = jnp.max(scores, axis=1, keepdims=True)
+            exps = jnp.exp2((scores - largest) * (math.log2(math.e) / math.sqrt(HD)))
+            scale = 1.0 / jnp.sum(exps, axis=1, keepdims=True)
+            mixed = jnp.dot(exps.astype(jnp.bfloat16), values, preferred_element_type=jnp.float32)
+            mixed = mixed * scale
+            for i in range(PAIR):
+                piece = jnp.where(valid, mixed[i * BLOCK : (i + 1) * BLOCK], 0.0)
+                place = order[j] * half_q + h * head_span + (r + i) * HD
+                ctx_out[part, pl.ds(pl.multiple_of(place, HD), HD)] = piece.astype(jnp.bfloat16)
+        return 0
 
     def caches(j):
         units_arrive(j, 2)
@@ -530,14 +514,12 @@
         for m in range(MAXB):
             place = m * BLOCK + lax.broadcasted_iota(jnp.int32, (BLOCK, HD), 0)
             for h in range(2):
-                for kv, out in ((0, kc), (1, vc)):
+                column = pl.ds(pl.multiple_of((order[j] * 2 + h) * HD, HD), HD)
+                for kv, out in ((0, key_out), (1, value_out)):
                     block = homes[j][2 * h + kv, m]
-                    out[j, pl.ds(m * BLOCK, BLOCK), pl.ds(h * HD, HD)] = jnp.where(
+                    out[0, pl.ds(m * BLOCK, BLOCK), column] = jnp.where(
                         place < length, block, jnp.zeros_like(block)
                     )
-        column = pl.ds(pl.multiple_of(order[j] * 2 * HD, 128), 2 * HD)
-        copy_out("keys", kc.at[j], key_out.at[0, :, column], 7 + 2 * j)
-        copy_out("values", vc.at[j], value_out.at[0, :, column], 8 + 2 * j)
 
     for dz in NEAR:
         multiply(dz)
@@ -579,8 +561,6 @@
     give_picked(1)
     attend(1)
     caches(1)
-    for copy in outs.values():
-        copy.wait()
     for conditions, copy in sends:
         when_all(conditions, copy.wait_send)
 
@@ -595,16 +575,17 @@
     total = seq_of_slot.shape[0]
     plane = 4 * rows
     dma = pltpu.SemaphoreType.DMA
-    anywhere = pl.BlockSpec(memory_space=pl.ANY)
+    anywhere = pl.BlockSpec(memory_space=pltpu.HBM)
+    vmem = pl.BlockSpec(memory_space=pltpu.VMEM)
     smem = pl.BlockSpec(memory_space=pltpu.SMEM)
-    cache = jax.ShapeDtypeStruct((1, MAXB * BLOCK, local_heads * HD), jnp.bfloat16)
     bf16, f32 = jnp.bfloat16, jnp.float32
+    cache = pltpu.VMEM((1, MAXB * BLOCK, local_heads * HD), bf16)
     half_q = queries.shape[1] // 2
     return pl.pallas_call(
         functools.partial(rebuild_kernel, depth),
-        out_shape=(jax.ShapeDtypeStruct(queries.shape, bf16), cache, cache),
+        out_shape=(pltpu.VMEM(queries.shape, bf16), cache, cache),
         in_specs=[anywhere] * 4 + [smem] * 3,
-        out_specs=(anywhere,) * 3,
+        out_specs=(vmem,) * 3,
         scratch_shapes=[
             pltpu.VMEM((4, rows, half), bf16),
             pltpu.VMEM((depth, 4 * wide, half), bf16),
@@ -621,13 +602,9 @@
             pltpu.VMEM((4, 4, BLOCK, HD), bf16),
             pltpu.VMEM((4, 4, BLOCK, HD), bf16),
             pltpu.VMEM((2, rows, half_q), bf16),
-            pltpu.VMEM((rows, half_q), bf16),
-            pltpu.VMEM((rows, half_q), bf16),
-            pltpu.VMEM((2, MAXB * BLOCK, 2 * HD), bf16),
-            pltpu.VMEM((2, MAXB * BLOCK, 2 * HD), bf16),
             pltpu.VMEM((plane, HD), f32),
             pltpu.VMEM((plane, HD), f32),
-            dma((11,)),
+            dma((5,)),
             dma((128,)),
             dma((4 * depth,)),
             dma((4 * PIECES,)),
@@ -637,7 +614,7 @@
             dma((18,)),
         ],
         compiler_params=pltpu.CompilerParams(
-            collective_id=0, has_side_effects=True, vmem_limit_bytes=60 * 2**20
+            collective_id=0, has_side_effects=True, vmem_limit_bytes=62300 * 2**10
         ),
     )(hidden, w_key.T, w_value.T, queries, lengths, seq_of_slot, pos_of_slot)
 

time: 140 us -> 132 us (0.943)
  Pallas kernels: 134 us -> 129 us
  local copies, waits for them, and re-layouts: 4.81 us -> 2.91 us
    pallas_call x1, Pallas kernels: 134 us -> 129 us  [fast_shards(): pl.pallas_call(functools.partial(rebuild_kernel, depth), out_shape=(pltpu...]
    unnamed x7 -> x3, local copies, waits for them, and re-layouts: 4.81 us -> 2.91 us
where the time goes in v2:
time: 132 us
  Pallas kernels  129 us (98%)
  local copies, waits for them, and re-layouts  2.91 us (2%)
    pallas_call x1, Pallas kernels, fast_shards(): pl.pallas_call(functools.partial(rebuild_kernel, depth), out_shape=(pltpu...  129 us
    unnamed x3, local copies, waits for them, and re-layouts  2.91 us

profile of v2, /device:TPU:0, one launch (start us, length us, event | category | flops | bytes accessed | tf_op | source)
XLA Modules:
  0.0 132.1 jit_solution(5336196522589883434)
XLA Ops:
  0.6 128.6 %shard_map.94 = (bf16[256,4096]{1,0:T(8,128)(2,1)S(1)}, bf16[1,512,512]{2,1,0:T(8,128)(2,1)S(1)}, bf16[1,512,512]{2,1,0:T(8,128)(2,1)S(1)}) custom-call(bf16[256,4096]{1,0:T(8,128)(2,1)} %hidden_ref.1, bf16[64,4096]{1,0:T(8,128)(2,1)} %bitcast.2, bf16[64,4096]{1,0:T(8,128)(2,1)} %bitcast.3, bf16[256,4096]{1,0:T(8,128)(2,1)} %q_ref.1, s32[16]{0:T(128)} %len_ref.1, ...), custom_call_target="tpu_custom_call" | custom-call | tf_op jit(solution)/shard_map/pallas_call | solution.py:584
  129.2 1.3 %copy.13 = bf16[256,4096]{1,0:T(8,128)(2,1)} copy(bf16[256,4096]{1,0:T(8,128)(2,1)S(1)} %get-tuple-element.3) | data formatting | bytes 4194304
  130.5 0.8 copy.14
  131.3 0.8 copy.15

commit v3 on v2

--- a/solution.py
+++ b/solution.py
@@ -140,6 +140,8 @@
     xr,
     kv0,
     kv1,
+    kv2,
+    kv3,
     sel,
     home_sel,
     arr0,
@@ -167,7 +169,8 @@
     rows = hidden_ref.shape[0]
     feats = hid.shape[2]
     wide = wk_ref.shape[0]
-    kvs = (kv0, kv1)
+    kvs = (kv0, kv1, kv2, kv3)
+    half = BLOCK // 2
     arrs = (arr0, arr1)
     homes = (home0, home1)
     slots = rows // BLOCK
@@ -210,6 +213,7 @@
     def send(conditions, src, dst, sem, device):
         copy = remote(src, dst, sem, device)
         sends.append((conditions, copy))
+        assert len(sends) <= send_sem.shape[0]
         when_all(conditions, copy.start)
 
     def arrived(conditions, dst, sem):
@@ -389,81 +393,94 @@
         outer = 1 - ((zc + 1) // 2) % 2
         arrived([exists(dz), owner(dz) == core], xr.at[k], x_recv.at[k])
         for j in range(2):
-            kv = kvs[j]
-            mine_here = [exists(dz), owner(dz) == core, outer == j]
-
-            def body(kv=kv, j=j):
+
+            def body(j=j):
+                def store(i, block):
+                    for p in range(2):
+                        kvs[2 * j + p][z * plane_slots + i] = block[p * half : (p + 1) * half].astype(
+                            jnp.bfloat16
+                        )
+
                 for i in range(plane_slots):
                     part = pl.ds(i * BLOCK, BLOCK)
                     total = acc[zc, x, part] + peer[k, x, part] + xr[k, part].astype(jnp.float32)
 
                     def turn(total=total, part=part, i=i):
-                        turned = total * cos_t[part] + pltpu.roll(total, HD // 2, 1) * sin_t[part]
-                        kv[z * plane_slots + i] = turned.astype(jnp.bfloat16)
-
-                    def keep(total=total, i=i):
-                        kv[z * plane_slots + i] = total.astype(jnp.bfloat16)
+                        store(i, total * cos_t[part] + pltpu.roll(total, HD // 2, 1) * sin_t[part])
 
                     pl.when(x == 0)(turn)
-                    pl.when(x != 0)(keep)
-
-            when_all(mine_here, body)
-            block = kv.at[pl.ds(z * plane_slots, plane_slots)]
-            send(mine_here + [up()], block, block, z_recv.at[j * depth + z], to_z(1))
-            send(mine_here + [down()], block, block, z_recv.at[j * depth + z], to_z(-1))
-
-    def kv_arrive(j, dz):
-        here = exists(dz)
-        block = kvs[j].at[pl.ds((z + dz) * plane_slots, plane_slots)]
-        sem = z_recv.at[j * depth + z + dz]
+                    pl.when(x != 0)(functools.partial(store, i, total))
+
+            when_all([exists(dz), owner(dz) == core, outer == j], body)
+
+    def kv_part(p, plane):
+        return kvs[p].at[pl.ds(plane * plane_slots, plane_slots)], z_recv.at[p * depth + plane]
+
+    def own_sends(p, conditions):
+        block, sem = kv_part(p, z)
+        send(conditions + [up()], block, block, sem, to_z(1))
+        send(conditions + [down()], block, block, sem, to_z(-1))
+
+    def relay(p, dz, condition):
+        block, sem = kv_part(p, z + dz)
         sign = 1 if dz < 0 else -1
-        onward = up() if sign > 0 else down()
-        arrived([here, onward], block, sem)
-        if abs(dz) < depth - 1:
-            send([here, onward], block, block, sem, to_z(sign))
-
-    def kv_last(j, dz):
-        sign = 1 if dz < 0 else -1
-        onward = up() if sign > 0 else down()
-        block = kvs[j].at[pl.ds((z + dz) * plane_slots, plane_slots)]
-        arrived([exists(dz), jnp.logical_not(onward)], block, z_recv.at[j * depth + z + dz])
-
-    def unit_sem(j, t, kind):
-        return u_recv.at[(j * 3 + t) * 3 + kind]
-
-    def give_own(j):
+        conditions = [condition, exists(dz), up() if sign > 0 else down()]
+        arrived(conditions, block, sem)
+        send(conditions, block, block, sem, to_z(sign))
+
+    def relays(p):
+        low = z * 2 < depth
+        high = jnp.logical_not(low)
+        for near, dz in ((1, 1), (-1, 1), (1, 2)):
+            relay(p, near * dz, low)
+            relay(p, -near * dz, high)
+
+    def last(p):
+        for dz in range(1, depth):
+            for sign in (1, -1):
+                block, sem = kv_part(p, z - sign * dz)
+                onward = up() if sign > 0 else down()
+                arrived([exists(-sign * dz), jnp.logical_not(onward)], block, sem)
+
+    def unit_sem(p, t, kind):
+        return u_recv.at[(p * 3 + t) * 3 + kind]
+
+    def part_rows(p):
+        return pl.ds(p % 2 * half, half)
+
+    def landing(p, src, kind):
+        return (homes if kind == 2 else arrs)[p // 2].at[src, pl.ds(*UNITS[kind]), part_rows(p)]
+
+    def give_own(p):
         for t in range(3):
-            src = kvs[j].at[pl.ds(z * plane_slots + plane_ids[t] * slots, slots)]
-            send([], src, arrs[j].at[mine, pl.ds(0, slots)], unit_sem(j, t, 0), targets[t])
-        arrs[j][mine, pl.ds(0, slots)] = kvs[j][pl.ds(me * slots, slots)]
-
-    def landing(j, src, kind):
-        return (homes if kind == 2 else arrs)[j].at[src, pl.ds(*UNITS[kind])]
-
-    def give_picked(j):
-        kv = kvs[j]
+            src = kvs[p].at[pl.ds(z * plane_slots + plane_ids[t] * slots, slots)]
+            send([], src, landing(p, mine, 0), unit_sem(p, t, 0), targets[t])
+        arrs[p // 2][mine, pl.ds(0, slots), part_rows(p)] = kvs[p][pl.ds(me * slots, slots)]
+
+    def give_picked(p):
+        kv, j, part = kvs[p], p // 2, part_rows(p)
         for kind, staged in ((1, sel), (2, home_sel)):
             for t in range(3):
                 for u in range(UNITS[kind][1]):
-                    staged[j, t, u] = kv[picks[t][kind - 1][u]]
-                send([], staged.at[j, t], landing(j, mine, kind), unit_sem(j, t, kind), targets[t])
+                    staged[j, t, u, part] = kv[picks[t][kind - 1][u]]
+                send([], staged.at[j, t, :, part], landing(p, mine, kind), unit_sem(p, t, kind), targets[t])
         for u in range(UNITS[1][1]):
-            arrs[j][mine, UNITS[1][0] + u] = kv[picks[3][0][u]]
+            arrs[j][mine, UNITS[1][0] + u, part] = kv[picks[3][0][u]]
         for u in range(UNITS[2][1]):
-            homes[j][mine, u] = kv[picks[3][1][u]]
-
-    def units_arrive(j, kind):
-        for t in range(3):
-            arrived([], landing(j, plane_ids[t], kind), unit_sem(j, t, kind))
+            homes[j][mine, u, part] = kv[picks[3][1][u]]
+
+    def units_arrive(j, sources, kinds):
+        for p in (2 * j, 2 * j + 1):
+            for t in sources:
+                for kind in kinds:
+                    arrived([], landing(p, plane_ids[t], kind), unit_sem(p, t, kind))
 
     ratio = half_q // (2 * HD)
     head_span = ratio * HD
-    def attend(j):
-        for part, head in ((0, y), (1, 1 - y)):
-            for t in range(3)[part : 2 * part + 1]:
-                for kind in range(2):
-                    arrived([], landing(j, plane_ids[t], kind), unit_sem(j, t, kind))
-            lax.fori_loop(0, slots, functools.partial(attend_head, j, head), 0)
+    def attend(j, part):
+        units_arrive(j, (1, 2) if part else (0,), (0, 1))
+        head = 1 - y if part else y
+        lax.fori_loop(0, slots, functools.partial(attend_head, j, head), 0)
 
     def attend_head(j, h, s, _):
         earlier = MAXB - 1
@@ -509,7 +526,7 @@
         return 0
 
     def caches(j):
-        units_arrive(j, 2)
+        units_arrive(j, range(3), (2,))
         length = len_ref[me]
         for m in range(MAXB):
             place = m * BLOCK + lax.broadcasted_iota(jnp.int32, (BLOCK, HD), 0)
@@ -535,9 +552,13 @@
         reduce(dz)
     for dz in (-2, 2):
         finish(dz)
+    edge = jnp.logical_not(inner)
+    own_sends(0, [])
     give_own(0)
-    for dz in (-1, 1, -2, 2):
-        kv_arrive(0, dz)
+    relays(0)
+    own_sends(1, [])
+    give_own(1)
+    relays(1)
     w_arrive(-3, 0)
     w_arrive(3, 0)
     w_arrive(-3, 1)
@@ -548,18 +569,24 @@
         reduce(dz)
     for dz in (-3, 3):
         finish(dz)
-    give_own(1)
-    for dz in (-1, 1, -2, 2, -3, 3):
-        kv_last(0, dz)
-    give_picked(0)
-    for dz in (-1, 1, -2, 2):
-        kv_arrive(1, dz)
-    attend(0)
+    for p in (2, 3):
+        own_sends(p, [edge])
+        give_own(p)
+    for p in (0, 1):
+        last(p)
+        give_picked(p)
+    for p in (2, 3):
+        own_sends(p, [inner])
+        relays(p)
+    attend(0, 0)
+    last(2)
+    give_picked(2)
+    attend(0, 1)
     caches(0)
-    for dz in (-1, 1, -2, 2, -3, 3):
-        kv_last(1, dz)
-    give_picked(1)
-    attend(1)
+    last(3)
+    give_picked(3)
+    attend(1, 0)
+    attend(1, 1)
     caches(1)
     for conditions, copy in sends:
         when_all(conditions, copy.wait_send)
@@ -593,8 +620,9 @@
             pltpu.VMEM((2, 2, plane, HD), f32),
             pltpu.VMEM((2, plane, HD), bf16),
             pltpu.VMEM((2, plane, HD), bf16),
-            pltpu.VMEM((total, BLOCK, HD), bf16),
-            pltpu.VMEM((total, BLOCK, HD), bf16),
+        ]
+        + [pltpu.VMEM((total, BLOCK // 2, HD), bf16)] * 4
+        + [
             pltpu.VMEM((2, 3, 6, BLOCK, HD), bf16),
             pltpu.VMEM((2, 3, 4, BLOCK, HD), bf16),
             pltpu.VMEM((4, 8, BLOCK, HD), bf16),
@@ -605,13 +633,13 @@
             pltpu.VMEM((plane, HD), f32),
             pltpu.VMEM((plane, HD), f32),
             dma((5,)),
-            dma((128,)),
+            dma((192,)),
             dma((4 * depth,)),
             dma((4 * PIECES,)),
             dma((2,)),
             dma((2,)),
-            dma((2 * depth,)),
-            dma((18,)),
+            dma((4 * depth,)),
+            dma((36,)),
         ],
         compiler_params=pltpu.CompilerParams(
             collective_id=0, has_side_effects=True, vmem_limit_bytes=62300 * 2**10

time: 132 us -> 128 us (0.970); the launches traced: 132 us -> 126 us
  Pallas kernels: 129 us -> 123 us
    pallas_call x1, Pallas kernels: 129 us -> 123 us  [fast_shards(): pl.pallas_call(functools.partial(rebuild_kernel, depth), out_shape=(pltpu...]
where the time goes in v3:
time: 128 us; the launch traced here: 126 us
  Pallas kernels  123 us (96%)
  local copies, waits for them, and re-layouts  2.91 us (2%)
    pallas_call x1, Pallas kernels, fast_shards(): pl.pallas_call(functools.partial(rebuild_kernel, depth), out_shape=(pltpu...  123 us
    unnamed x3, local copies, waits for them, and re-layouts  2.91 us

profile of v3, /device:TPU:0, one launch (start us, length us, event | category | flops | bytes accessed | tf_op | source)
XLA Modules:
  0.0 126.1 jit_solution(9724461530757411456)
XLA Ops:
  0.6 122.5 %shard_map.94 = (bf16[256,4096]{1,0:T(8,128)(2,1)S(1)}, bf16[1,512,512]{2,1,0:T(8,128)(2,1)S(1)}, bf16[1,512,512]{2,1,0:T(8,128)(2,1)S(1)}) custom-call(bf16[256,4096]{1,0:T(8,128)(2,1)} %hidden_ref.1, bf16[64,4096]{1,0:T(8,128)(2,1)} %bitcast.2, bf16[64,4096]{1,0:T(8,128)(2,1)} %bitcast.3, bf16[256,4096]{1,0:T(8,128)(2,1)} %q_ref.1, s32[16]{0:T(128)} %len_ref.1, ...), custom_call_target="tpu_custom_call" | custom-call | tf_op jit(solution)/shard_map/pallas_call | solution.py:611
  123.2 1.3 %copy.13 = bf16[256,4096]{1,0:T(8,128)(2,1)} copy(bf16[256,4096]{1,0:T(8,128)(2,1)S(1)} %get-tuple-element.3) | data formatting | bytes 4194304
  124.5 0.8 copy.14
  125.3 0.8 copy.15

commit v4 on v3

--- a/solution.py
+++ b/solution.py
@@ -105,6 +105,7 @@
 MESH = pl.DeviceIdType.MESH
 PIECES = 4
 PAIR = 2
+WRITES = 4
 NEAR = (0, -1, 1)
 UNITS = ((0, 2), (2, 6), (0, 4))
 
@@ -592,6 +593,17 @@
         when_all(conditions, copy.wait_send)
 
 
+def write_kernel(ctx_ref, key_ref, value_ref, ctx_out, key_out, value_out, sem):
+    step = ctx_ref.shape[0] // WRITES
+    pairs = [(ctx_ref.at[pl.ds(i * step, step)], ctx_out.at[pl.ds(i * step, step)]) for i in range(WRITES)]
+    pairs += [(key_ref, key_out), (value_ref, value_out)]
+    copies = [pltpu.make_async_copy(a, b, sem.at[i]) for i, (a, b) in enumerate(pairs)]
+    for copy in copies:
+        copy.start()
+    for copy in copies:
+        copy.wait()
+
+
 def fast_shards(hidden, w_key, w_value, queries, lengths, seq_of_slot, pos_of_slot):
     depth = lax.axis_size("dp") // 4
     rows, features = hidden.shape
@@ -608,7 +620,7 @@
     bf16, f32 = jnp.bfloat16, jnp.float32
     cache = pltpu.VMEM((1, MAXB * BLOCK, local_heads * HD), bf16)
     half_q = queries.shape[1] // 2
-    return pl.pallas_call(
+    found = pl.pallas_call(
         functools.partial(rebuild_kernel, depth),
         out_shape=(pltpu.VMEM(queries.shape, bf16), cache, cache),
         in_specs=[anywhere] * 4 + [smem] * 3,
@@ -645,6 +657,15 @@
             collective_id=0, has_side_effects=True, vmem_limit_bytes=62300 * 2**10
         ),
     )(hidden, w_key.T, w_value.T, queries, lengths, seq_of_slot, pos_of_slot)
+    free = pl.BlockSpec(memory_space=pl.ANY)
+    return pl.pallas_call(
+        write_kernel,
+        out_shape=tuple(jax.ShapeDtypeStruct(f.shape, f.dtype) for f in found),
+        in_specs=[vmem] * 3,
+        out_specs=(free,) * 3,
+        scratch_shapes=[dma((2 + WRITES,))],
+        compiler_params=pltpu.CompilerParams(vmem_limit_bytes=8 * 2**20),
+    )(*found)
 
 
 def suits(mesh):

time: 128 us -> 127 us (level)
  local copies, waits for them, and re-layouts: 2.91 us -> 0 us
    unnamed x3 -> x0, local copies, waits for them, and re-layouts: 2.91 us -> none
    pallas_call x0 -> x1, Pallas kernels: none -> 1.71 us  [fast_shards(): pl.pallas_call(write_kernel, out_shape=tuple((jax.ShapeDtypeStruct(f.shap...]
where the time goes in v4:
time: 127 us; the launch traced here: 125 us
  Pallas kernels  124 us (98%)
    pallas_call x1, Pallas kernels, fast_shards(): pl.pallas_call(functools.partial(rebuild_kernel, depth), out_shape=(pltpu...  123 us

profile of v4, /device:TPU:0, one launch (start us, length us, event | category | flops | bytes accessed | tf_op | source)
XLA Modules:
  0.0 125.0 jit_solution(3973847988479999695)
XLA Ops:
  0.6 122.5 %shard_map.94 = (bf16[256,4096]{1,0:T(8,128)(2,1)S(1)}, bf16[1,512,512]{2,1,0:T(8,128)(2,1)S(1)}, bf16[1,512,512]{2,1,0:T(8,128)(2,1)S(1)}) custom-call(bf16[256,4096]{1,0:T(8,128)(2,1)} %hidden_ref.1, bf16[64,4096]{1,0:T(8,128)(2,1)} %bitcast.2, bf16[64,4096]{1,0:T(8,128)(2,1)} %bitcast.3, bf16[256,4096]{1,0:T(8,128)(2,1)} %q_ref.1, s32[16]{0:T(128)} %len_ref.1, ...), custom_call_target="tpu_custom_call" | custom-call | tf_op jit(solution)/shard_map/pallas_call | solution.py:623
  123.2 1.7 %shard_map.95 = (bf16[256,4096]{1,0:T(8,128)(2,1)}, bf16[1,512,512]{2,1,0:T(8,128)(2,1)}, bf16[1,512,512]{2,1,0:T(8,128)(2,1)}) custom-call(bf16[256,4096]{1,0:T(8,128)(2,1)S(1)} %get-tuple-element.6.ctx_ref, bf16[1,512,512]{2,1,0:T(8,128)(2,1)S(1)} %get-tuple-element.7.key_ref, bf16[1,512,512]{2,1,0:T(8,128)(2,1)S(1)} %get-tuple-element.8.value_ref), custom_call_target="tpu_custom_call" | custom-call | tf_op jit(solution)/shard_map/pallas_call | solution.py:661

commit v5 on v4

--- a/solution.py
+++ b/solution.py
@@ -104,7 +104,7 @@
 
 MESH = pl.DeviceIdType.MESH
 PIECES = 4
-PAIR = 2
+PAIR = 4
 WRITES = 4
 NEAR = (0, -1, 1)
 UNITS = ((0, 2), (2, 6), (0, 4))

time: 127 us -> 125 us (0.984)
  no operation moved by 1% of the time
where the time goes in v5:
time: 125 us; the launch traced here: 124 us
  Pallas kernels  123 us (98%)
    pallas_call x1, Pallas kernels, fast_shards(): pl.pallas_call(functools.partial(rebuild_kernel, depth), out_shape=(pltpu...  121 us

profile of v5, /device:TPU:0, one launch (start us, length us, event | category | flops | bytes accessed | tf_op | source)
XLA Modules:
  0.0 123.8 jit_solution(10053956557044073757)
XLA Ops:
  0.6 121.3 %shard_map.94 = (bf16[256,4096]{1,0:T(8,128)(2,1)S(1)}, bf16[1,512,512]{2,1,0:T(8,128)(2,1)S(1)}, bf16[1,512,512]{2,1,0:T(8,128)(2,1)S(1)}) custom-call(bf16[256,4096]{1,0:T(8,128)(2,1)} %hidden_ref.1, bf16[64,4096]{1,0:T(8,128)(2,1)} %bitcast.2, bf16[64,4096]{1,0:T(8,128)(2,1)} %bitcast.3, bf16[256,4096]{1,0:T(8,128)(2,1)} %q_ref.1, s32[16]{0:T(128)} %len_ref.1, ...), custom_call_target="tpu_custom_call" | custom-call | tf_op jit(solution)/shard_map/pallas_call | solution.py:623
  122.0 1.7 %shard_map.95 = (bf16[256,4096]{1,0:T(8,128)(2,1)}, bf16[1,512,512]{2,1,0:T(8,128)(2,1)}, bf16[1,512,512]{2,1,0:T(8,128)(2,1)}) custom-call(bf16[256,4096]{1,0:T(8,128)(2,1)S(1)} %get-tuple-element.6.ctx_ref, bf16[1,512,512]{2,1,0:T(8,128)(2,1)S(1)} %get-tuple-element.7.key_ref, bf16[1,512,512]{2,1,0:T(8,128)(2,1)S(1)} %get-tuple-element.8.value_ref), custom_call_target="tpu_custom_call" | custom-call | tf_op jit(solution)/shard_map/pallas_call | solution.py:661
